TPU v7x, 32 devices: a whole 2x2x4 slice. The times are simulated.
32 devices in a mesh: enc: 8 (over z, x), tp: 4 (over y, core).
Axes of the slice: x: 2, y: 2, z: 4, core: 2. Of those that a mesh axis runs over, the one named last changes fastest.
Arguments:
- grad_rows: bfloat16 [3072, 8192], P('enc', 'tp'), may hold values from -6 to 6
- features: bfloat16 [3072, 1280], P('enc'), may hold values from -6 to 6
- block_in: bfloat16 [3072, 1280], P('enc', 'tp'), may hold values from -6 to 6
- patch_counts: int32 [8, 3], replicated, may hold values from 32 to 128, as said below
- owner: int32 [8, 3], replicated, may hold values from 0 to 7, as said below
- ln1_gain: float32 [1280], replicated, may hold values from 0.5 to 1.5
- w_qkv: bfloat16 [1280, 16, 240], P(None, 'tp')
- w_out: bfloat16 [1280, 1280], P('tp'), may hold values from -0.15625 to 0.15625
- w_proj: bfloat16 [1280, 8192], P(None, 'tp'), may hold values from -0.15625 to 0.15625
Outputs:
- grad_input: bfloat16 [3072, 1280], P('enc', 'tp')
- grad_proj: float32 [1280, 8192], P('enc', 'tp')
- grad_qkv: float32 [1280, 16, 240], P('enc', 'tp')
- grad_out: float32 [1280, 1280], P('tp', 'enc')
- grad_ln1: float32 [1280], P('enc')
Inputs may be any that keep to these rules, and one draw needn't show every extreme that they name: `patch_counts`: some image has exactly 128 live rows and some exactly 32. `owner`: each encoder device receives exactly 3 images, never two from the same block.
All inputs are finite; a program needn't handle non-finite values.
Results may differ from a plain program's by a relative error of at most 0.033.
Values may be sent and summed in bfloat16 or wider, within the bound.
A program may use at most 64 MiB of HBM per device.

v0:
```python
import jax
import jax.numpy as jnp
from jax import lax
from jax.sharding import PartitionSpec as P

TILE = 128
EPSILON = 1e-05


def shortened(shard):

    def short(part):
        return part.astype(jnp.bfloat16) if part.dtype == jnp.float32 else part

    return jax.tree.map(short, shard)


def normalize(values):
    centred = values - jnp.mean(values, axis=-1, keepdims=True)
    variance = jnp.mean(centred * centred, axis=-1, keepdims=True)
    inverse = lax.rsqrt(variance + EPSILON)
    return (centred * inverse, inverse)


def norm_back(incoming, normed, inverse, gain):
    scaled = incoming * gain
    inner_mean = jnp.mean(scaled * normed, axis=-1, keepdims=True)
    outgoing = inverse * (scaled - jnp.mean(scaled, axis=-1, keepdims=True) - normed * inner_mean)
    return (outgoing, jnp.sum(incoming * normed, axis=0))


def dot_nt(left, right):
    return lax.dot_general(
        left, right, (((1,), (1,)), ((), ())), preferred_element_type=jnp.float32
    )


def dot_tn(left, right):
    return lax.dot_general(
        left, right, (((0,), (0,)), ((), ())), preferred_element_type=jnp.float32
    )


def shards(grad_rows, features, block_in, patch_counts, owner, ln1_gain, w_qkv, w_out, w_proj):
    groups = lax.axis_size("enc")
    device = lax.axis_index("enc")
    tp_rank = lax.axis_index("tp")
    block_rows = grad_rows.shape[0]
    img_group = block_rows // TILE
    block_full = lax.all_gather(block_in, "tp", axis=1, tiled=True)
    line_index = jnp.arange(TILE, dtype=jnp.int32)
    peer_index = jnp.arange(groups, dtype=jnp.int32)
    own_counts = lax.dynamic_index_in_dim(patch_counts, device, 0, keepdims=False)
    own_owner = lax.dynamic_index_in_dim(owner, device, 0, keepdims=False)
    live_own = line_index[None, :] < own_counts[:, None]

    def outgoing(row_block):
        columns = row_block.shape[1]
        tiles = row_block.reshape(img_group, TILE, columns)
        tiles = jnp.where(live_own[:, :, None], tiles, jnp.zeros_like(tiles))
        return jnp.zeros((groups, TILE, columns), row_block.dtype).at[own_owner].set(tiles)

    sends = jnp.any(owner == device, axis=1)
    sends_int = sends.astype(jnp.int32)
    rank = jnp.cumsum(sends_int) - sends_int
    slot_index = jnp.arange(img_group, dtype=jnp.int32)
    source_of = jnp.sum(
        jnp.where(sends[None, :] & (rank[None, :] == slot_index[:, None]), peer_index[None, :], 0),
        axis=1,
    )
    source_owner = jnp.take(owner, source_of, axis=0)
    source_counts = jnp.take(patch_counts, source_of, axis=0)
    arrived_counts = jnp.sum(jnp.where(source_owner == device, source_counts, 0), axis=1)
    live_tiles = line_index[None, :] < arrived_counts[:, None]
    shared = lax.psum_scatter(
        dot_nt(grad_rows, w_proj).astype(jnp.bfloat16), "tp", scatter_dimension=1, tiled=True
    ).astype(jnp.float32)
    received = lax.all_to_all(
        outgoing(shared).astype(jnp.bfloat16), "enc", split_axis=0, concat_axis=0, tiled=True
    ).astype(jnp.float32)
    vis_grad = lax.all_gather(
        shortened(jnp.take(received, source_of, axis=0).reshape(block_rows, received.shape[2])),
        "tp",
        axis=1,
        tiled=True,
    )
    kept_rows = jnp.where(live_own.reshape(-1)[:, None], features, jnp.zeros_like(features))
    proj_term = dot_tn(kept_rows, grad_rows)
    features_dim = block_full.shape[1]
    heads_here = w_qkv.shape[1]
    head_size = w_qkv.shape[2] // 3
    rows_here = block_full.shape[0]
    qkv_flat = w_qkv.reshape(features_dim, heads_here * 3 * head_size)
    normed1, inverse1 = normalize(block_full.astype(jnp.float32))
    normed_in = (normed1 * ln1_gain).astype(jnp.bfloat16)
    packed = jnp.dot(normed_in, qkv_flat, preferred_element_type=jnp.float32).astype(jnp.bfloat16)
    packed = packed.reshape(img_group, TILE, heads_here, 3, head_size)
    queries = packed[:, :, :, 0, :]
    keys_part = packed[:, :, :, 1, :]
    values_part = packed[:, :, :, 2, :]
    scaling = 1.0 / head_size**0.5
    scores = (
        jnp.einsum("gqhd,gkhd->ghqk", queries, keys_part, preferred_element_type=jnp.float32)
        * scaling
    )
    same_kind = (live_tiles[:, :, None] == live_tiles[:, None, :])[:, None]
    scores = jnp.where(same_kind, scores, -1e30)
    row_max = jnp.max(scores, axis=-1, keepdims=True)
    exp_terms = jnp.exp(scores - row_max)
    probability = exp_terms / jnp.sum(exp_terms, axis=-1, keepdims=True)
    prob_low = probability.astype(jnp.bfloat16)
    mixed = jnp.einsum(
        "ghqk,gkhd->gqhd", prob_low, values_part, preferred_element_type=jnp.float32
    ).astype(jnp.bfloat16)
    mixed = mixed.reshape(rows_here, heads_here * head_size)
    middle_b = vis_grad.astype(jnp.bfloat16)
    out_term = dot_tn(mixed, middle_b)
    mixed_grad = (
        dot_nt(middle_b, w_out).astype(jnp.bfloat16).reshape(img_group, TILE, heads_here, head_size)
    )
    prob_grad = jnp.einsum(
        "gqhd,gkhd->ghqk", mixed_grad, values_part, preferred_element_type=jnp.float32
    )
    score_grad = (
        probability
        * (prob_grad - jnp.sum(probability * prob_grad, axis=-1, keepdims=True))
        * scaling
    )
    score_grad = score_grad.astype(jnp.bfloat16)
    q_grad = jnp.einsum(
        "ghqk,gkhd->gqhd", score_grad, keys_part, preferred_element_type=jnp.float32
    )
    k_grad = jnp.einsum("ghqk,gqhd->gkhd", score_grad, queries, preferred_element_type=jnp.float32)
    v_grad = jnp.einsum("ghqk,gqhd->gkhd", prob_low, mixed_grad, preferred_element_type=jnp.float32)
    packed_grad = jnp.stack([q_grad, k_grad, v_grad], axis=3).astype(jnp.bfloat16)
    packed_grad = packed_grad.reshape(rows_here, heads_here * 3 * head_size)
    qkv_term = dot_tn(normed_in, packed_grad).reshape(features_dim, heads_here, 3 * head_size)
    in_part = dot_nt(packed_grad, qkv_flat)
    share_width = features_dim // lax.axis_size("tp")
    share_start = tp_rank * share_width
    in_sum = lax.psum(in_part.astype(jnp.bfloat16), "tp").astype(jnp.float32)
    in_back, ln1_term = norm_back(in_sum, normed1, inverse1, ln1_gain)
    grad_full = (vis_grad + in_back).astype(jnp.bfloat16)
    grad_input = lax.dynamic_slice_in_dim(grad_full, share_start, share_width, 1)
    grad_proj, grad_qkv, grad_out, grad_ln1 = (
        lax.psum_scatter(
            proj_term.astype(jnp.bfloat16), "enc", scatter_dimension=0, tiled=True
        ).astype(jnp.float32),
        lax.psum_scatter(
            qkv_term.astype(jnp.bfloat16), "enc", scatter_dimension=0, tiled=True
        ).astype(jnp.float32),
        lax.psum_scatter(
            out_term.astype(jnp.bfloat16), "enc", scatter_dimension=1, tiled=True
        ).astype(jnp.float32),
        lax.psum_scatter(
            ln1_term.astype(jnp.bfloat16), "enc", scatter_dimension=0, tiled=True
        ).astype(jnp.float32),
    )
    return (grad_input, grad_proj, grad_qkv, grad_out, grad_ln1)


def solution(mesh):
    placed = (
        P("enc", "tp"),
        P("enc", None),
        P("enc", "tp"),
        P(),
        P(),
        P(),
        P(None, "tp", None),
        P("tp", None),
        P(None, "tp"),
    )
    return jax.shard_map(
        shards,
        mesh=mesh,
        in_specs=placed,
        out_specs=(P("enc", "tp"), P("enc", "tp"), P("enc", "tp", None), P("tp", "enc"), P("enc")),
        check_vma=False,
    )
```

profile of v0, /device:TPU:0, one launch (start us, length us, event | category | flops | bytes accessed | tf_op | source)
XLA Modules:
  0.0 404.1 jit_solution(6433689965465876006)
XLA Ops:
  7.2 7.0 %convolution_convert_fusion.4 = bf16[384,1280]{0,1:T(8,128)(2,1)} fusion(bf16[384,2048]{1,0:T(8,128)(2,1)} %param.11, bf16[1280,2048]{1,0:T(8,128)(2,1)} %param.19), kind=kOutput, calls=%fused_computation.10 | convolution fusion | flops 2013757440 | bytes 7798784 | tf_op jit(solution)/shard_map/dot_general | solution.py:33
  14.6 11.6 %all_gather.7 = bf16[384,1280]{0,1:T(8,128)(2,1)} all-gather(bf16[384,320]{0,1:T(8,128)(2,1)S(1)} %copy-done.5), channel_id=1, replica_groups=mesh['enc'=8,'tp'=4] {'tp'}, dimensions={1}, use_global_device_ids=true | all-gather | bytes 1228800 | tf_op jit(solution)/shard_map/all_gather | solution.py:50
  26.2 1.6 copy.120
  29.7 2.5 convolution_convert_fusion.5
  32.2 3.2 reshape.234
  35.9 5.7 %reduce-scatter.5.cloned.1.call-done = bf16[384,320]{0,1:T(8,128)(2,1)} async-done(((bf16[384,1280]{0,1:T(8,128)(2,1)}), bf16[384,320]{0,1:T(8,128)(2,1)}) %reduce-scatter.5.cloned.1.call-update) | async-done | bytes 245776 | tf_op jit(solution)/shard_map/reduce_scatter | solution.py:75
  41.6 1.9 copy.115
  43.5 2.0 broadcast_select_fusion
  45.5 2.1 copy.116
  47.6 1.2 broadcast_in_dim.100
  48.7 2.7 scatter_fusion
  51.4 2.3 convert_element_type.112
  53.7 5.5 %all-to-all-start = ((bf16[8,128,320]{1,2,0:T(8,128)(2,1)}), bf16[8,128,320]{1,2,0:T(8,128)(2,1)}, u32[]{:S(2)}, u32[]{:S(2)}) async-start(bf16[8,128,320]{1,2,0:T(8,128)(2,1)} %convert_element_type.112), calls=%async_computation.1 | async-start | bytes 1310720 | tf_op jit(solution)/shard_map/all_to_all | solution.py:78
  59.5 2.4 fusion.52
  61.9 2.4 fusion.53
  64.3 12.2 %all-to-all-done = bf16[8,128,320]{1,2,0:T(8,128)(2,1)} async-done(((bf16[8,128,320]{1,2,0:T(8,128)(2,1)}), bf16[8,128,320]{1,2,0:T(8,128)(2,1)}, u32[]{:S(2)}, u32[]{:S(2)}) %all-to-all-start) | async-done | bytes 655392 | tf_op jit(solution)/shard_map/all_to_all | solution.py:78
  76.5 2.4 gather_fusion
  78.8 1.8 copy.117
  80.6 1.8 copy.118
  82.5 1.0 select_convert_fusion
  83.4 8.7 %all_gather.6 = bf16[384,1280]{0,1:T(8,128)(2,1)S(1)} all-gather(bf16[384,320]{0,1:T(8,128)(2,1)S(1)} %select_convert_fusion), channel_id=1, replica_groups=mesh['enc'=8,'tp'=4] {'tp'}, dimensions={1}, use_global_device_ids=true | all-gather | bytes 1228800 | tf_op jit(solution)/shard_map/all_gather | solution.py:81
  92.2 1.1 copy-done.1
  93.2 2.4 convolution_convert_fusion.6
  95.6 1.7 reshape.235
  97.4 2.3 fusion.34
  99.7 2.3 convolution_bitcast_fusion
  102.0 3.1 convolution_bitcast_fusion.2
  105.1 3.1 convolution_bitcast_fusion.1
  108.3 1.3 maximum_convert_fusion
  110.3 0.9 copy-done.3
  111.2 2.2 convolution_convert_fusion.3
  113.6 1.6 fusion.13
  115.5 1.7 convolution_convert_fusion.2
  117.3 4.4 %convolution_convert_fusion.1 = bf16[1280,4,240]{2,0,1:T(8,128)(2,1)} fusion(bf16[4,240,384]{2,1,0:T(8,128)(2,1)} %bitcast.97, f32[1280]{0:T(1024)S(1)} %copy-done.7, bf16[384,1280]{1,0:T(8,128)(2,1)S(1)} %copy.120, f32[384]{0:T(512)S(1)} %add_rsqrt_fusion, f32[384]{0:T(512)S(1)} %broadcast_multiply_fusion.2), kind=kOutput, calls=%fused_computation.7 | convolution fusion | flops 947404800 | bytes 4186112 | tf_op jit(solution)/shard_map/dot_general | solution.py:39
  121.8 7.1 %convolution_convert_fusion = bf16[1280,2048]{1,0:T(8,128)(2,1)} fusion(bf16[384,2048]{1,0:T(8,128)(2,1)} %param.11, bf16[384,1280]{1,0:T(8,128)(2,1)} %param.12, pred[384]{0:T(512)(128)(4,1)S(1)} %get-tuple-element.44), kind=kOutput, calls=%fused_computation.6 | convolution fusion | flops 2016378880 | bytes 7799168 | tf_op jit(solution)/shard_map/dot_general | solution.py:39
  130.8 1.7 constant_dynamic-slice_fusion
  132.4 1.8 copy.146
  134.3 14.2 %all-reduce.3.cloned.1.call-done = bf16[384,1280]{1,0:T(8,128)(2,1)} async-done(((bf16[384,1280]{1,0:T(8,128)(2,1)}), bf16[384,1280]{1,0:T(8,128)(2,1)}) %all-reduce.3.cloned.1.call-update) | async-done | bytes 983056 | tf_op jit(solution)/shard_map/psum | solution.py:141
  148.5 2.2 fusion.5
  151.3 0.9 copy.135
  152.2 21.4 %all-reduce = bf16[1280]{0:T(1024)(128)(2,1)S(1)} all-reduce(bf16[1280]{0:T(1024)(128)(2,1)S(1)} %get-tuple-element.36), channel_id=6, replica_groups=mesh['enc'=8,'tp'=4] {'enc'}, use_global_device_ids=true, to_apply=%region_18.20.clone | all-reduce | flops 1280 | bytes 5120
  173.5 0.6 dynamic-slice_convert_fusion
  174.2 42.1 %reduce-scatter.11.cloned.1.call-done = bf16[320,160]{0,1:T(8,128)(2,1)} async-done(((bf16[320,1280]{0,1:T(8,128)(2,1)}), bf16[320,160]{0,1:T(8,128)(2,1)}) %reduce-scatter.11.cloned.1.call-update) | async-done | bytes 102416 | tf_op jit(solution)/shard_map/reduce_scatter | solution.py:152
  216.3 1.6 convert_element_type.134
  217.9 71.7 %reduce-scatter.9.cloned.1.call-done = bf16[160,4,240]{2,0,1:T(8,128)(2,1)} async-done(((bf16[1280,4,240]{2,0,1:T(8,128)(2,1)}), bf16[160,4,240]{2,0,1:T(8,128)(2,1)}) %reduce-scatter.9.cloned.1.call-update) | async-done | bytes 307216 | tf_op jit(solution)/shard_map/reduce_scatter | solution.py:149
  289.7 2.1 copy.136
  291.7 103.6 %reduce-scatter.7.cloned.1.call-done = bf16[160,2048]{1,0:T(8,128)(2,1)} async-done(((bf16[1280,2048]{1,0:T(8,128)(2,1)}), bf16[160,2048]{1,0:T(8,128)(2,1)}) %reduce-scatter.7.cloned.1.call-update) | async-done | bytes 655376 | tf_op jit(solution)/shard_map/reduce_scatter | solution.py:146
  395.3 2.3 convert_element_type.128
  (60 shorter events, 6.3 us)
Async XLA Ops:
  7.2 22.6 %copy-start = (bf16[1280,4,240]{0,2,1:T(8,128)(2,1)S(1)}, bf16[1280,4,240]{0,2,1:T(8,128)(2,1)}, u32[]{:S(2)}) copy-start(bf16[1280,4,240]{0,2,1:T(8,128)(2,1)} %param.17) | copy-start | bytes 7372804
  7.2 7.1 %copy-start.6 = (s32[8,3]{0,1:T(4,128)S(1)}, s32[8,3]{0,1:T(4,128)}, u32[]{:S(2)}) copy-start(s32[8,3]{0,1:T(4,128)} %param.15) | copy-start | bytes 292
  7.2 7.4 %copy-start.5 = (bf16[384,320]{0,1:T(8,128)(2,1)S(1)}, bf16[384,320]{0,1:T(8,128)(2,1)}, u32[]{:S(2)}) copy-start(bf16[384,320]{0,1:T(8,128)(2,1)} %param.13) | copy-start | bytes 737284
  7.2 34.4 %reduce-scatter.5.cloned.1.call-start = ((), (), s32[]{:S(2)}) async-start(), calls=%async_computation.5 | async-start | bytes 1228800 | tf_op jit(solution)/shard_map/reduce_scatter | solution.py:75
  14.6 13.5 %copy-start.8 = (s32[8,3]{0,1:T(4,128)S(1)}, s32[8,3]{0,1:T(4,128)}, u32[]{:S(2)}) copy-start(s32[8,3]{0,1:T(4,128)} %param.14) | copy-start | bytes 292
  26.2 3.5 copy-start.7
  53.7 22.8 %all-to-all-start = ((bf16[8,128,320]{1,2,0:T(8,128)(2,1)}), bf16[8,128,320]{1,2,0:T(8,128)(2,1)}, u32[]{:S(2)}, u32[]{:S(2)}) async-start(bf16[8,128,320]{1,2,0:T(8,128)(2,1)} %convert_element_type.112), calls=%async_computation.1 | async-start | bytes 1310720 | tf_op jit(solution)/shard_map/all_to_all | solution.py:78
  59.2 89.3 %all-reduce.3.cloned.1.call-start = ((), (), s32[]{:S(2)}) async-start(), calls=%async_computation.6 | async-start | bytes 1966080 | tf_op jit(solution)/shard_map/psum | solution.py:141
  92.2 1.1 copy-start.1
  110.3 0.9 copy-start.3
  113.4 102.9 %reduce-scatter.11.cloned.1.call-start = ((), (), s32[]{:S(2)}) async-start(), calls=%async_computation.9 | async-start | bytes 1105920 | tf_op jit(solution)/shard_map/reduce_scatter | solution.py:152
  113.6 1.8 copy-start.2
  117.3 172.4 %reduce-scatter.9.cloned.1.call-start = ((), (), s32[]{:S(2)}) async-start(), calls=%async_computation.8 | async-start | bytes 2949120 | tf_op jit(solution)/shard_map/reduce_scatter | solution.py:149
  121.8 273.5 %reduce-scatter.7.cloned.1.call-start = ((), (), s32[]{:S(2)}) async-start(), calls=%async_computation.7 | async-start | bytes 5898240 | tf_op jit(solution)/shard_map/reduce_scatter | solution.py:146
  128.9 0.7 copy-start.9
  148.5 2.3 copy-start.4
Sparse Core Ops, SparseCore 0:
  14.4 27.1 reduce-scatter.4
  113.5 34.9 all-reduce.2
  151.8 64.4 reduce-scatter.10
  219.7 69.9 reduce-scatter.8
  293.1 102.1 reduce-scatter.6
where the time goes:
time: 405 us; the launch traced here: 404 us
  waiting for transfers between devices  250 us (62%)
  matrix products  42.2 us (10%)
  blocking collectives  41.7 us (10%)
  local copies, waits for them, and re-layouts  34.8 us (9%)
  other arithmetic  15.3 us (4%)
  between operations  14.7 us (4%)
  starting transfers between devices  5.9 us (1%)
    reduce_scatter x1, waiting for transfers between devices, shards(): lax.psum_scatter(proj_term.astype(jnp.bfloat16), 'enc', scatter_dimension...  104 us
    reduce_scatter x1, waiting for transfers between devices, shards(): lax.psum_scatter(qkv_term.astype(jnp.bfloat16), 'enc', scatter_dimension=...  71.7 us
    reduce_scatter x1, waiting for transfers between devices, shards(): lax.psum_scatter(out_term.astype(jnp.bfloat16), 'enc', scatter_dimension=...  42.1 us
    unnamed x1, blocking collectives  21.4 us
    psum x1, waiting for transfers between devices, shards(): in_sum = lax.psum(in_part.astype(jnp.bfloat16), 'tp').astype(jnp.float32)  14.2 us
    dot_general x3, matrix products, dot_tn(): lax.dot_general(left, right, (((0,), (0,)), ((), ())), preferred_element_...  13.2 us
    all_to_all x1, waiting for transfers between devices, shards(): lax.all_to_all(outgoing(shared).astype(jnp.bfloat16), 'enc', split_axis=0...  12.2 us
    all_gather x1, blocking collectives, shards(): block_full = lax.all_gather(block_in, 'tp', axis=1, tiled=True)  11.6 us
  transfers between devices with their start and end apart: 6, of which 6 were waited for; matrix products, arithmetic and copies ran while one was open for 10% of the time, Pallas kernels for 0%

commit v1 on v0

--- a/solution.py
+++ b/solution.py
@@ -138,7 +138,7 @@
     in_part = dot_nt(packed_grad, qkv_flat)
     share_width = features_dim // lax.axis_size("tp")
     share_start = tp_rank * share_width
-    in_sum = lax.psum(in_part.astype(jnp.bfloat16), "tp").astype(jnp.float32)
+    in_sum = jnp.sum(lax.all_gather(in_part.astype(jnp.bfloat16), "tp"), axis=0).astype(jnp.float32)
     in_back, ln1_term = norm_back(in_sum, normed1, inverse1, ln1_gain)
     grad_full = (vis_grad + in_back).astype(jnp.bfloat16)
     grad_input = lax.dynamic_slice_in_dim(grad_full, share_start, share_width, 1)

time: 405 us -> 383 us (0.946)
  waiting for transfers between devices: 250 us -> 223 us
    all_gather x0 -> x1, waiting for transfers between devices: none -> 31.5 us  [shards(): lax.all_gather(in_part.astype(jnp.bfloat16), 'tp')]
    reduce_scatter x1, waiting for transfers between devices: 104 us -> 76.2 us  [shards(): lax.psum_scatter(proj_term.astype(jnp.bfloat16), 'enc', scatter_dimension...]
    reduce_scatter x1, waiting for transfers between devices: 42.1 us -> 27.4 us  [shards(): lax.psum_scatter(out_term.astype(jnp.bfloat16), 'enc', scatter_dimension=...]
    psum x1 -> x0, waiting for transfers between devices: 14.2 us -> none  [shards(): in_sum = lax.psum(in_part.astype(jnp.bfloat16), 'tp').astype(jnp.float32)]
    unnamed x27 -> x29, local copies, waits for them, and re-layouts: 8.21 us -> 8.11 us
  transfers between devices with their start and end apart: 6 -> 6, of which waited for: 6 -> 6; matrix products, arithmetic and copies ran while one was open for 10% -> 16% of each run, Pallas kernels for 0% -> 0%
where the time goes in v1:
time: 383 us; the launch traced here: 382 us
  waiting for transfers between devices  223 us (58%)
  matrix products  42.6 us (11%)
  blocking collectives  42.5 us (11%)
  local copies, waits for them, and re-layouts  35.4 us (9%)
  other arithmetic  18 us (5%)
  between operations  14.7 us (4%)
  starting transfers between devices  5.89 us (2%)
    reduce_scatter x1, waiting for transfers between devices, shards(): lax.psum_scatter(proj_term.astype(jnp.bfloat16), 'enc', scatter_dimension...  76.2 us
    reduce_scatter x1, waiting for transfers between devices, shards(): lax.psum_scatter(qkv_term.astype(jnp.bfloat16), 'enc', scatter_dimension=...  72 us
    all_gather x1, waiting for transfers between devices, shards(): lax.all_gather(in_part.astype(jnp.bfloat16), 'tp')  31.5 us
    reduce_scatter x1, waiting for transfers between devices, shards(): lax.psum_scatter(out_term.astype(jnp.bfloat16), 'enc', scatter_dimension=...  27.4 us
    unnamed x1, blocking collectives  22.2 us
    dot_general x3, matrix products, dot_nt(): lax.dot_general(left, right, (((1,), (1,)), ((), ())), preferred_element_...  13 us
    dot_general x3, matrix products, dot_tn(): lax.dot_general(left, right, (((0,), (0,)), ((), ())), preferred_element_...  13 us
    all_to_all x1, waiting for transfers between devices, shards(): lax.all_to_all(outgoing(shared).astype(jnp.bfloat16), 'enc', split_axis=0...  12.1 us
  transfers between devices with their start and end apart: 6, of which 6 were waited for; matrix products, arithmetic and copies ran while one was open for 16% of the time, Pallas kernels for 0%

profile of v1, /device:TPU:0, one launch (start us, length us, event | category | flops | bytes accessed | tf_op | source)
XLA Modules:
  0.0 381.7 jit_solution(17743417379007356578)
XLA Ops:
  7.3 7.0 %convolution_convert_fusion.4 = bf16[384,1280]{0,1:T(8,128)(2,1)} fusion(bf16[384,2048]{1,0:T(8,128)(2,1)} %param.11, bf16[1280,2048]{1,0:T(8,128)(2,1)} %param.19), kind=kOutput, calls=%fused_computation.10 | convolution fusion | flops 2013757440 | bytes 7798784 | tf_op jit(solution)/shard_map/dot_general | solution.py:33
  14.8 11.6 %all_gather.13 = bf16[384,1280]{0,1:T(8,128)(2,1)} all-gather(bf16[384,320]{0,1:T(8,128)(2,1)S(1)} %copy-done.4), channel_id=1, replica_groups=mesh['enc'=8,'tp'=4] {'tp'}, dimensions={1}, use_global_device_ids=true | all-gather | bytes 1228800 | tf_op jit(solution)/shard_map/all_gather | solution.py:50
  26.4 1.6 copy.114
  29.7 2.5 convolution_convert_fusion.5
  32.2 3.2 reshape.234
  35.9 2.4 fusion.52
  38.3 3.2 reduce-scatter.5.cloned.1.call-done
  41.5 1.9 copy.109
  43.5 2.0 broadcast_select_fusion
  45.5 2.1 copy.110
  47.5 1.2 broadcast_in_dim.100
  48.7 2.7 scatter_fusion
  51.4 2.3 convert_element_type.114
  53.6 5.5 %all-to-all-start = ((bf16[8,128,320]{1,2,0:T(8,128)(2,1)}), bf16[8,128,320]{1,2,0:T(8,128)(2,1)}, u32[]{:S(2)}, u32[]{:S(2)}) async-start(bf16[8,128,320]{1,2,0:T(8,128)(2,1)} %convert_element_type.114), calls=%async_computation.1 | async-start | bytes 1310720 | tf_op jit(solution)/shard_map/all_to_all | solution.py:78
  59.3 2.4 fusion.53
  61.7 1.5 fusion.13
  63.3 0.9 copy.128
  64.3 12.1 %all-to-all-done = bf16[8,128,320]{1,2,0:T(8,128)(2,1)} async-done(((bf16[8,128,320]{1,2,0:T(8,128)(2,1)}), bf16[8,128,320]{1,2,0:T(8,128)(2,1)}, u32[]{:S(2)}, u32[]{:S(2)}) %all-to-all-start) | async-done | bytes 655392 | tf_op jit(solution)/shard_map/all_to_all | solution.py:78
  76.4 2.4 gather_fusion
  78.8 1.8 copy.111
  80.6 1.8 copy.112
  82.4 1.0 select_convert_fusion
  83.4 8.7 %all_gather.12 = bf16[384,1280]{0,1:T(8,128)(2,1)S(1)} all-gather(bf16[384,320]{0,1:T(8,128)(2,1)S(1)} %select_convert_fusion), channel_id=1, replica_groups=mesh['enc'=8,'tp'=4] {'tp'}, dimensions={1}, use_global_device_ids=true | all-gather | bytes 1228800 | tf_op jit(solution)/shard_map/all_gather | solution.py:81
  92.1 0.9 copy-done.1
  93.0 2.7 convolution_convert_fusion.2
  96.0 2.7 convolution_convert_fusion.6
  98.8 1.7 reshape.235
  100.5 2.3 fusion.34
  102.8 3.1 convolution_bitcast_fusion.2
  105.9 3.1 convolution_bitcast_fusion.1
  109.0 1.7 convolution_bitcast_fusion
  111.6 0.9 copy-done.2
  112.4 3.3 convolution_convert_fusion.1
  115.7 3.3 convolution_convert_fusion.3
  119.2 7.0 %convolution_convert_fusion = bf16[1280,2048]{1,0:T(8,128)(2,1)} fusion(bf16[384,2048]{1,0:T(8,128)(2,1)} %param.11, bf16[384,1280]{1,0:T(8,128)(2,1)} %param.12, pred[384]{0:T(512)(128)(4,1)S(1)} %get-tuple-element.44), kind=kOutput, calls=%fused_computation.6 | convolution fusion | flops 2016378880 | bytes 7799168 | tf_op jit(solution)/shard_map/dot_general | solution.py:39
  128.1 1.7 constant_dynamic-slice_fusion
  129.8 1.9 copy.140
  131.6 27.4 %reduce-scatter.11.cloned.1.call-done = bf16[320,160]{0,1:T(8,128)(2,1)} async-done(((bf16[320,1280]{0,1:T(8,128)(2,1)}), bf16[320,160]{0,1:T(8,128)(2,1)}) %reduce-scatter.11.cloned.1.call-update) | async-done | bytes 102416 | tf_op jit(solution)/shard_map/reduce_scatter | solution.py:152
  159.0 1.6 convert_element_type.136
  160.6 72.0 %reduce-scatter.9.cloned.1.call-done = bf16[160,4,240]{2,0,1:T(8,128)(2,1)} async-done(((bf16[1280,4,240]{2,0,1:T(8,128)(2,1)}), bf16[160,4,240]{2,0,1:T(8,128)(2,1)}) %reduce-scatter.9.cloned.1.call-update) | async-done | bytes 307216 | tf_op jit(solution)/shard_map/reduce_scatter | solution.py:149
  232.6 2.1 copy.130
  234.7 31.5 %all-gather.3.cloned.1.call-done = bf16[1536,1280]{1,0:T(8,128)(2,1)} async-done(((bf16[384,1280]{1,0:T(8,128)(2,1)}), bf16[1536,1280]{1,0:T(8,128)(2,1)}) %all-gather.3.cloned.1.call-update) | async-done | bytes 3932176 | tf_op jit(solution)/shard_map/all_gather | solution.py:141
  266.2 3.9 %reduce_sum.102 = bf16[384,1280]{1,0:T(8,128)(2,1)} reduce(bf16[4,384,1280]{2,1,0:T(8,128)(2,1)} %bitcast.96, bf16[]{:T(256)} %constant.70.clone.1), dimensions={0}, to_apply=%region_11.13 | reduce | flops 1474560 | bytes 4915202 | tf_op jit(solution)/shard_map/reduce_sum | solution.py:141
  270.1 2.2 fusion.5
  272.9 0.9 copy.129
  273.8 22.2 %all-reduce = bf16[1280]{0:T(1024)(128)(2,1)S(1)} all-reduce(bf16[1280]{0:T(1024)(128)(2,1)S(1)} %get-tuple-element.36), channel_id=7, replica_groups=mesh['enc'=8,'tp'=4] {'enc'}, use_global_device_ids=true, to_apply=%region_18.20.clone | all-reduce | flops 1280 | bytes 5120
  296.6 76.2 %reduce-scatter.7.cloned.1.call-done = bf16[160,2048]{1,0:T(8,128)(2,1)} async-done(((bf16[1280,2048]{1,0:T(8,128)(2,1)}), bf16[160,2048]{1,0:T(8,128)(2,1)}) %reduce-scatter.7.cloned.1.call-update) | async-done | bytes 655376 | tf_op jit(solution)/shard_map/reduce_scatter | solution.py:146
  372.9 2.3 convert_element_type.130
  (63 shorter events, 6.8 us)
Async XLA Ops:
  7.2 22.5 %copy-start = (bf16[1280,4,240]{0,2,1:T(8,128)(2,1)S(1)}, bf16[1280,4,240]{0,2,1:T(8,128)(2,1)}, u32[]{:S(2)}) copy-start(bf16[1280,4,240]{0,2,1:T(8,128)(2,1)} %param.17) | copy-start | bytes 7372804
  7.2 7.1 %copy-start.7 = (s32[8,3]{0,1:T(4,128)S(1)}, s32[8,3]{0,1:T(4,128)}, u32[]{:S(2)}) copy-start(s32[8,3]{0,1:T(4,128)} %param.15) | copy-start | bytes 292
  7.2 7.5 %copy-start.9 = (s32[8,3]{0,1:T(4,128)S(1)}, s32[8,3]{0,1:T(4,128)}, u32[]{:S(2)}) copy-start(s32[8,3]{0,1:T(4,128)} %param.14) | copy-start | bytes 292
  7.2 7.6 %copy-start.4 = (bf16[384,320]{0,1:T(8,128)(2,1)S(1)}, bf16[384,320]{0,1:T(8,128)(2,1)}, u32[]{:S(2)}) copy-start(bf16[384,320]{0,1:T(8,128)(2,1)} %param.13) | copy-start | bytes 737284
  7.2 34.3 %reduce-scatter.5.cloned.1.call-start = ((), (), s32[]{:S(2)}) async-start(), calls=%async_computation.5 | async-start | bytes 1228800 | tf_op jit(solution)/shard_map/reduce_scatter | solution.py:75
  26.4 3.3 copy-start.8
  53.6 22.8 %all-to-all-start = ((bf16[8,128,320]{1,2,0:T(8,128)(2,1)}), bf16[8,128,320]{1,2,0:T(8,128)(2,1)}, u32[]{:S(2)}, u32[]{:S(2)}) async-start(bf16[8,128,320]{1,2,0:T(8,128)(2,1)} %convert_element_type.114), calls=%async_computation.1 | async-start | bytes 1310720 | tf_op jit(solution)/shard_map/all_to_all | solution.py:78
  59.2 99.9 %reduce-scatter.11.cloned.1.call-start = ((), (), s32[]{:S(2)}) async-start(), calls=%async_computation.8 | async-start | bytes 1105920 | tf_op jit(solution)/shard_map/reduce_scatter | solution.py:152
  92.1 0.9 copy-start.1
  95.8 136.8 %reduce-scatter.9.cloned.1.call-start = ((), (), s32[]{:S(2)}) async-start(), calls=%async_computation.7 | async-start | bytes 2949120 | tf_op jit(solution)/shard_map/reduce_scatter | solution.py:149
  109.0 1.7 copy-start.5
  109.0 1.7 copy-start.6
  111.5 0.9 copy-start.2
  115.7 150.5 %all-gather.3.cloned.1.call-start = ((), (), s32[]{:S(2)}) async-start(), calls=%async_computation.9 | async-start | bytes 4915200 | tf_op jit(solution)/shard_map/all_gather | solution.py:141
  119.1 253.7 %reduce-scatter.7.cloned.1.call-start = ((), (), s32[]{:S(2)}) async-start(), calls=%async_computation.6 | async-start | bytes 5898240 | tf_op jit(solution)/shard_map/reduce_scatter | solution.py:146
  126.2 0.7 copy-start.10
  270.1 2.3 copy-start.3
Sparse Core Ops, SparseCore 0:
  14.4 27.1 reduce-scatter.4
  95.9 63.0 reduce-scatter.10
  162.6 69.9 reduce-scatter.8
  234.0 32.1 all-gather.2
  269.6 103.2 reduce-scatter.6
